TPU v7x, 256 devices: a whole 4x4x8 slice. The times are simulated.
256 devices in a mesh: grp: 32 (over x, z), sub: 8 (over y, core).
Axes of the slice: x: 4, y: 4, z: 8, core: 2. Of those that a mesh axis runs over, the one named last changes fastest.
Arguments:
- ham_columns: bfloat16 [768, 5, 128, 128], P(('grp', 'sub')), may hold values from -2.2 to 2.2, as said below
- bond_mask: int32 [768, 4], P(('grp', 'sub')), may hold values 0 or 1
- owned_counts: int32 [32, 8], replicated, may hold values from 1 to 3, as said below
- fermi_level: float32 [1], replicated, may hold values from -0.5 to 0.5
Outputs:
- density: bfloat16 [768, 9, 128, 128], P(('grp', 'sub'))
Inputs may be any that keep to these rules, and one draw needn't show every extreme that they name: `ham_columns`: block 0 of every stored block column is symmetric. `bond_mask`: bond lists of slots that hold no cluster are never read. `owned_counts`: along sub, the devices 2k and 2k + 1 of a group own 2 * 2 block columns together, so group g owns clusters g * 16 to (g + 1) * 16 - 1, handed to its devices in order along sub in consecutive runs; no device owns exactly 2; every row has a device that owns 3.
All inputs are finite; a program needn't handle non-finite values. No bound on the sum of `bond_mask` on one device may be relied on, other than what follows from the above.
Results may differ from a plain program's by a relative error of at most 0.0025.
Values may be sent and summed in bfloat16 or wider, within the bound.
No kernel may reach another device: no remote copies, remote signals or barrier semaphores. Data moves between devices by JAX's collectives and lax.ppermute only.
A program may use at most 64 MiB of HBM per device.

v0:
```python
import jax
import jax.numpy as jnp
from jax import lax
from jax.sharding import PartitionSpec as P

COLS_MEAN = 2
spectral_span = 4.0


def extended(array, sides, width):
    for axis, dim in sides:
        size, length = (lax.axis_size(axis), array.shape[dim])
        up = [(i, (i + 1) % size) for i in range(size)]
        down = [(j, i) for i, j in up]
        last = lax.slice_in_dim(array, length - width, length, axis=dim)
        leading = lax.slice_in_dim(array, 0, width, axis=dim)
        before = lax.ppermute(last, axis, up)
        after = lax.ppermute(leading, axis, down)
        array = jnp.concatenate([before, array, after], axis=dim)
    return array


def partner(value, axis, distance):
    mask = 2**distance
    pairs = [(source, source ^ mask) for source in range(lax.axis_size(axis))]
    return lax.ppermute(value, axis, pairs)


def build_tile(window_cols, window_bonds, chemical):
    reach_len = window_bonds.shape[1]
    window_len = window_cols.shape[0]
    block_width = window_cols.shape[2]
    identity = jnp.eye(block_width, dtype=jnp.float32)
    bond_values = window_bonds.astype(jnp.float32)
    living = []
    for member in range(window_len):
        if member == reach_len:
            living.append(jnp.ones((), jnp.float32))
        elif member > reach_len:
            living.append(bond_values[reach_len, member - reach_len - 1])
        else:
            living.append(bond_values[member, reach_len - member - 1])
    rows_list = []
    for row_blk in range(window_len):
        pieces = []
        for col_blk in range(window_len):
            distance = row_blk - col_blk
            weight = living[row_blk] * living[col_blk]
            if distance == 0:
                block_value = (
                    window_cols[row_blk, 0].astype(jnp.float32) - chemical * identity
                ) * weight
            elif 0 < distance <= reach_len:
                block_value = window_cols[col_blk, distance].astype(jnp.float32) * (
                    weight * bond_values[col_blk, distance - 1]
                )
            elif 0 < -distance <= reach_len:
                block_value = window_cols[row_blk, -distance].astype(jnp.float32).T * (
                    weight * bond_values[row_blk, -distance - 1]
                )
            else:
                block_value = jnp.zeros((block_width, block_width), jnp.float32)
            pieces.append(block_value)
        rows_list.append(jnp.concatenate(pieces, axis=1))
    return (jnp.concatenate(rows_list, axis=0) / spectral_span).astype(jnp.bfloat16)


def product(matrix, vector):
    return jnp.dot(matrix, vector.astype(jnp.bfloat16), preferred_element_type=jnp.float32)


def apply_rest(matrix, first_term):
    second = product(matrix, first_term)
    third_term = product(matrix, second)
    return 1.5 * first_term - 0.5 * third_term


def density_column(matrix, window_len, block_width):
    center = (window_len - 1) // 2
    first_term = matrix[:, center * block_width : (center + 1) * block_width].astype(jnp.float32)
    step_one = apply_rest(matrix, first_term)
    step_two = apply_rest(matrix, product(matrix, step_one))
    step_three = apply_rest(matrix, product(matrix, step_two))
    sign_column = 1.5 * step_one - 0.5 * step_three
    above = jnp.zeros((center * block_width, block_width), jnp.float32)
    selector = jnp.concatenate([above, jnp.eye(block_width, dtype=jnp.float32), above], axis=0)
    result = (0.5 * (selector - sign_column)).astype(jnp.bfloat16)
    return result.reshape(window_len, block_width, block_width)


def window_result(run_cols, run_bonds, first_row, chemical):
    window_len = 2 * run_bonds.shape[1] + 1
    block_width = run_cols.shape[2]
    window_cols = lax.dynamic_slice_in_dim(run_cols, first_row, window_len, 0)
    window_bonds = lax.dynamic_slice_in_dim(run_bonds, first_row, window_len, 0)
    matrix = build_tile(window_cols, window_bonds, chemical)
    return density_column(matrix, window_len, block_width)


def body(ham_columns, bond_mask, owned_counts, fermi_level):
    reach_len = bond_mask.shape[1]
    slots_here = ham_columns.shape[0]
    group_size = lax.axis_size("sub")
    chemical = fermi_level[0]
    counts_flat = owned_counts.reshape(-1)
    group_index = lax.axis_index("grp")
    member_index = lax.axis_index("sub")
    device_index = group_index * group_size + member_index
    my_count = counts_flat[device_index]
    slot_range = jnp.arange(slots_here, dtype=jnp.int32)
    in_use = slot_range < my_count
    gathered_cols, gathered_bonds = (
        lax.all_gather(ham_columns, "sub", axis=0, tiled=True),
        lax.all_gather(bond_mask, "sub", axis=0, tiled=True),
    )
    group_counts = lax.dynamic_index_in_dim(owned_counts, group_index, 0, keepdims=False)
    group_ends = jnp.cumsum(group_counts)
    group_starts = group_ends - group_counts
    group_cols = COLS_MEAN * group_size
    positions = jnp.arange(group_cols, dtype=jnp.int32)
    owner_index = jnp.sum((group_ends[None, :] <= positions[:, None]).astype(jnp.int32), axis=1)
    gather_index = owner_index * slots_here + positions - group_starts[owner_index]
    local_cols = jnp.take(gathered_cols, gather_index, axis=0)
    local_bonds = jnp.take(gathered_bonds, gather_index, axis=0)
    edge_cols, edge_bonds = (
        extended(local_cols, (("grp", 0),), reach_len),
        extended(local_bonds, (("grp", 0),), reach_len),
    )
    first_rows = member_index * COLS_MEAN + jnp.arange(COLS_MEAN, dtype=jnp.int32)
    results = lax.map(
        lambda first_row: window_result(edge_cols, edge_bonds, first_row, chemical), first_rows
    )
    partner_results = partner(results, "sub", 0)
    is_odd = member_index % 2
    lower_first = jnp.concatenate([results, partner_results], axis=0)
    upper_first = jnp.concatenate([partner_results, results], axis=0)
    pair_results = jnp.where(is_odd == 0, lower_first, upper_first)
    pair_start = (member_index - is_odd) * COLS_MEAN
    wanted = jnp.minimum(group_starts[member_index] - pair_start + slot_range, 2 * COLS_MEAN - 1)
    picked = jnp.take(pair_results, wanted, axis=0)
    return jnp.where(in_use[:, None, None, None], picked, jnp.zeros_like(picked))


def solution(mesh):
    placed = (P(("grp", "sub"), None, None, None), P(("grp", "sub"), None), P(), P())
    return jax.shard_map(
        body,
        mesh=mesh,
        in_specs=placed,
        out_specs=P(("grp", "sub"), None, None, None),
        check_vma=False,
    )
```

profile of v0, /device:TPU:1, one launch (start us, length us, event | category | flops | bytes accessed | tf_op | source)
XLA Modules:
  0.0 367.3 jit_solution(13713588425739931471)
XLA Ops:
  8.3 14.4 %all-gather = s32[8,3,4]{2,1,0:T(4,128)S(1)} all-gather(s32[1,3,4]{2,1,0:T(4,128)} %bitcast.405), channel_id=1, replica_groups=mesh['grp'=32,'sub'=8] {'sub'}, dimensions={0}, use_global_device_ids=true | all-gather | bytes 432 | tf_op jit(solution)/shard_map/all_gather | solution.py:114
  24.2 22.8 %all-gather.3.cloned.1.call-done = bf16[24,5,128,128]{3,2,1,0:T(8,128)(2,1)} async-done(((bf16[3,5,128,128]{3,2,1,0:T(8,128)(2,1)}), bf16[24,5,128,128]{3,2,1,0:T(8,128)(2,1)}) %all-gather.3.cloned.1.call-update) | async-done | bytes 3932176 | tf_op jit(solution)/shard_map/all_gather | solution.py:113
  46.9 4.5 %gather_fusion.1 = bf16[16,5,128,128]{3,2,1,0:T(8,128)(2,1)} fusion(bf16[24,5,128,128]{3,2,1,0:T(8,128)(2,1)} %all-gather.3.cloned.1.call-done, s32[1024]{0:T(1024)S(1)} %pad_clamp_fusion.1), kind=kCustom, calls=%fused_computation.1 | custom fusion | bytes 5242944 | tf_op jit(solution)/shard_map/jit(_take)/gather | solution.py:123
  51.4 2.1 broadcast_select_fusion
  54.5 5.2 %collective-permute-start.1 = (bf16[4,5,128,128]{3,2,1,0:T(8,128)(2,1)}, bf16[4,5,128,128]{3,2,1,0:T(8,128)(2,1)}, u32[]{:S(2)}, u32[]{:S(2)}) collective-permute-start(bf16[4,5,128,128]{3,2,1,0:T(8,128)(2,1)} %get-tuple-element.119), channel_id=1, source_target_pairs={{8,0},{16,8},{24,16},{32,24},{40,32},{48,40},{56,48},{64,56},{72,6... | collective-permute-start | bytes 1966088 | tf_op jit(solution)/shard_map/ppermute | solution.py:18
  59.7 4.8 %collective-permute-start.3 = (s32[4,4]{1,0:T(4,128)S(1)}, s32[4,4]{1,0:T(4,128)S(1)}, u32[]{:S(2)}, u32[]{:S(2)}) collective-permute-start(s32[4,4]{1,0:T(4,128)S(1)} %get-tuple-element.121), channel_id=1, source_target_pairs={{8,0},{16,8},{24,16},{32,24},{40,32},{48,40},{56,48},{64,56},{72,6... | collective-permute-start | bytes 200 | tf_op jit(solution)/shard_map/ppermute | solution.py:18
  64.6 9.2 %collective-permute-done.3 = s32[4,4]{1,0:T(4,128)S(1)} collective-permute-done((s32[4,4]{1,0:T(4,128)S(1)}, s32[4,4]{1,0:T(4,128)S(1)}, u32[]{:S(2)}, u32[]{:S(2)}) %collective-permute-start.3) | collective-permute-done | bytes 96 | tf_op jit(solution)/shard_map/ppermute | solution.py:18
  73.8 5.0 %collective-permute-done.2 = s32[4,4]{1,0:T(4,128)S(1)} collective-permute-done((s32[4,4]{1,0:T(4,128)S(1)}, s32[4,4]{1,0:T(4,128)S(1)}, u32[]{:S(2)}, u32[]{:S(2)}) %collective-permute-start.2) | collective-permute-done | bytes 96 | tf_op jit(solution)/shard_map/ppermute | solution.py:17
  79.0 3.3 pad_maximum_fusion
  82.3 270.8 %while.10 = (s32[]{:T(128)}, bf16[2,9,128,128]{3,2,1,0:T(8,128)(2,1)}, s32[2]{0:T(128)S(1)}, bf16[24,5,128,128]{3,2,1,0:T(8,128)(2,1)}, f32[]{:T(128)}, /*index=...) while((s32[]{:T(128)}, ...), condition=%wide.region_3.4_spmd, body=%wide.region_2.3_spmd.sunk | while | flops 2726674432 | bytes 48746780 | solution.py:130
  86.9 2.1 constant_dynamic-update-slice_fusion.81
  110.8 1.4 constant_dynamic-update-slice_fusion.86
  112.2 2.1 fusion.119
  122.4 2.0 constant_dynamic-update-slice_fusion.90
  124.4 1.4 bitcast_dynamic-update-slice_fusion.44
  125.8 2.0 fusion.120
  158.8 1.4 constant_dynamic-update-slice_fusion.109
  160.2 1.4 bitcast_dynamic-update-slice_fusion.47
  161.6 1.4 bitcast_dynamic-update-slice_fusion.48
  163.0 1.4 bitcast_dynamic-update-slice_fusion.49
  164.4 2.1 fusion.122
  174.7 1.4 bitcast_dynamic-update-slice_fusion.54
  176.2 1.4 bitcast_dynamic-update-slice_fusion.55
  179.7 2.1 fusion.124
  186.7 1.4 bitcast_dynamic-update-slice_fusion.58
  188.1 1.4 bitcast_dynamic-update-slice_fusion.59
  189.5 2.1 fusion.126
  193.8 1.4 bitcast_dynamic-update-slice_fusion.60
  195.2 1.4 bitcast_dynamic-update-slice_fusion.61
  196.6 1.4 bitcast_dynamic-update-slice_fusion.62
  198.0 2.1 fusion.128
  200.0 2.9 multiply_convert_fusion.2
  203.6 3.3 fusion.130
  206.9 1.9 fusion.131
  209.7 3.3 fusion.132
  213.0 3.9 %fusion.133 = bf16[1152,128]{1,0:T(8,128)(2,1)S(1)} fusion(bf16[1152,1152]{1,0:T(8,128)(2,1)S(1)} %multiply_convert_fusion.2, f32[512,128]{1,0:T(8,128)S(1)} %broadcast.398, f32[128,128]{1,0:T(8,128)} %fusion.129, f32[1152,128]{1,0:T(8,128)} %fusion.132, f32[1152,128]{1,0:T(8,128)} %fusion.130), kind=kOutput, calls=%fused_computation.16.clone.1 | convolution fusion | flops 681394176 | bytes 4456448 | tf_op jit(solution)/shard_map/while/body/eval_jaxpr/dot_general | solution.py:69
  222.3 2.1 constant_dynamic-update-slice_fusion.81
  246.2 1.4 constant_dynamic-update-slice_fusion.86
  247.7 2.1 fusion.119
  257.8 2.0 constant_dynamic-update-slice_fusion.90
  259.9 1.4 bitcast_dynamic-update-slice_fusion.44
  261.3 2.0 fusion.120
  294.2 1.4 constant_dynamic-update-slice_fusion.109
  295.6 1.4 bitcast_dynamic-update-slice_fusion.47
  297.0 1.4 bitcast_dynamic-update-slice_fusion.48
  298.4 1.4 bitcast_dynamic-update-slice_fusion.49
  299.8 2.1 fusion.122
  310.2 1.4 bitcast_dynamic-update-slice_fusion.54
  311.6 1.4 bitcast_dynamic-update-slice_fusion.55
  315.1 2.1 fusion.124
  322.1 1.4 bitcast_dynamic-update-slice_fusion.58
  323.5 1.4 bitcast_dynamic-update-slice_fusion.59
  324.9 2.1 fusion.126
  329.2 1.4 bitcast_dynamic-update-slice_fusion.60
  330.6 1.4 bitcast_dynamic-update-slice_fusion.61
  332.0 1.4 bitcast_dynamic-update-slice_fusion.62
  333.4 2.1 fusion.128
  335.5 2.9 multiply_convert_fusion.2
  339.0 3.3 fusion.130
  342.3 1.9 fusion.131
  345.1 3.3 fusion.132
  348.4 3.9 %fusion.133 = bf16[1152,128]{1,0:T(8,128)(2,1)S(1)} fusion(bf16[1152,1152]{1,0:T(8,128)(2,1)S(1)} %multiply_convert_fusion.2, f32[512,128]{1,0:T(8,128)S(1)} %broadcast.398, f32[128,128]{1,0:T(8,128)} %fusion.129, f32[1152,128]{1,0:T(8,128)} %fusion.132, f32[1152,128]{1,0:T(8,128)} %fusion.130), kind=kOutput, calls=%fused_computation.16.clone.1 | convolution fusion | flops 681394176 | bytes 4456448 | tf_op jit(solution)/shard_map/while/body/eval_jaxpr/dot_general | solution.py:69
  353.1 1.4 collective-permute-start.4
  357.2 1.5 maximum_select_fusion
  (221 shorter events, 86.3 us)
Async XLA Ops:
  6.5 40.4 %all-gather.3.cloned.1.call-start = ((), (), s32[]{:S(2)}) async-start(), calls=%async_computation | async-start | bytes 4423680 | tf_op jit(solution)/shard_map/all_gather | solution.py:113
  54.5 24.5 %collective-permute-start.1 = (bf16[4,5,128,128]{3,2,1,0:T(8,128)(2,1)}, bf16[4,5,128,128]{3,2,1,0:T(8,128)(2,1)}, u32[]{:S(2)}, u32[]{:S(2)}) collective-permute-start(bf16[4,5,128,128]{3,2,1,0:T(8,128)(2,1)} %get-tuple-element.119), channel_id=1, source_target_pairs={{8,0},{16,8},{24,16},{32,24},{40,32},{48,40},{56,48},{64,56},{72,6... | collective-permute-start | bytes 1966088 | tf_op jit(solution)/shard_map/ppermute | solution.py:18
  59.6 19.4 %collective-permute-start = (bf16[4,5,128,128]{3,2,1,0:T(8,128)(2,1)S(1)}, bf16[4,5,128,128]{3,2,1,0:T(8,128)(2,1)}, u32[]{:S(2)}, u32[]{:S(2)}) collective-permute-start(bf16[4,5,128,128]{3,2,1,0:T(8,128)(2,1)S(1)} %get-tuple-element.118), channel_id=1, source_target_pairs={{0,8},{8,16},{16,24},{24,32},{32,40},{40,48},{48,56},{56,64},{64,7... | collective-permute-start | bytes 1966088 | tf_op jit(solution)/shard_map/ppermute | solution.py:17
  59.7 14.1 %collective-permute-start.3 = (s32[4,4]{1,0:T(4,128)S(1)}, s32[4,4]{1,0:T(4,128)S(1)}, u32[]{:S(2)}, u32[]{:S(2)}) collective-permute-start(s32[4,4]{1,0:T(4,128)S(1)} %get-tuple-element.121), channel_id=1, source_target_pairs={{8,0},{16,8},{24,16},{32,24},{40,32},{48,40},{56,48},{64,56},{72,6... | collective-permute-start | bytes 200 | tf_op jit(solution)/shard_map/ppermute | solution.py:18
  64.5 14.3 %collective-permute-start.2 = (s32[4,4]{1,0:T(4,128)S(1)}, s32[4,4]{1,0:T(4,128)S(1)}, u32[]{:S(2)}, u32[]{:S(2)}) collective-permute-start(s32[4,4]{1,0:T(4,128)S(1)} %get-tuple-element.120), channel_id=1, source_target_pairs={{0,8},{8,16},{16,24},{24,32},{32,40},{40,48},{48,56},{56,64},{64,7... | collective-permute-start | bytes 200 | tf_op jit(solution)/shard_map/ppermute | solution.py:17
  82.3 272.2 %copy-start = (s32[32,8]{0,1:T(8,128)S(1)}, s32[32,8]{0,1:T(8,128)}, u32[]{:S(2)}) copy-start(s32[32,8]{0,1:T(8,128)} %param.8) | copy-start | bytes 3076
  353.1 4.1 %collective-permute-start.4 = (bf16[2,9,128,128]{3,2,1,0:T(8,128)(2,1)}, bf16[2,9,128,128]{3,2,1,0:T(8,128)(2,1)S(1)}, u32[]{:S(2)}, u32[]{:S(2)}) collective-permute-start(bf16[2,9,128,128]{3,2,1,0:T(8,128)(2,1)} %get-tuple-element.37), channel_id=1, source_target_pairs={{0,1},{1,0},{2,3},{3,2},{4,5},{5,4},{6,7},{7,6},{8,9},{9,8},{10,11... | collective-permute-start | bytes 1769480 | tf_op jit(solution)/shard_map/ppermute | solution.py:26
Sparse Core Ops, SparseCore 0:
  9.2 37.7 all-gather.2
where the time goes:
time: 374 us; the launch traced here: 367 us
  other arithmetic  116 us (31%)
  loops' own time  92.8 us (25%)
  local copies, waits for them, and re-layouts  54.5 us (15%)
  waiting for transfers between devices  37.6 us (10%)
  matrix products  26.7 us (7%)
  blocking collectives  14.4 us (4%)
  between operations  14.1 us (4%)
  starting transfers between devices  11.4 us (3%)
    another operation x1, loops' own time, body(): lax.map(lambda first_row: window_result(edge_cols, edge_bonds, first_row,...  92.8 us
    while x84, other arithmetic  90.3 us
    while x72, local copies, waits for them, and re-layouts  33.7 us
    dot_general x10, matrix products, product(): jnp.dot(matrix, vector.astype(jnp.bfloat16), preferred_element_type=jnp.f...  26.7 us
    all_gather x1, waiting for transfers between devices, body(): lax.all_gather(ham_columns, 'sub', axis=0, tiled=True)  22.8 us
    all_gather x1, blocking collectives, body(): lax.all_gather(bond_mask, 'sub', axis=0, tiled=True)  14.4 us
    ppermute x2, starting transfers between devices, extended(): after = lax.ppermute(leading, axis, down)  9.97 us
    ppermute x2, waiting for transfers between devices, extended(): after = lax.ppermute(leading, axis, down)  9.16 us
  transfers between devices with their start and end apart: 6, of which 3 were waited for; matrix products, arithmetic and copies ran while one was open for 1% of the time, Pallas kernels for 0%

commit v1 on v0

--- a/solution.py
+++ b/solution.py
@@ -5,6 +5,11 @@
 
 COLS_MEAN = 2
 spectral_span = 4.0
+
+
+def gather_by_exchange(value, axis, dim):
+    copies = jnp.concatenate([value] * lax.axis_size(axis), axis=dim)
+    return lax.all_to_all(copies, axis, dim, dim, tiled=True)
 
 
 def extended(array, sides, width):
@@ -110,7 +115,7 @@
     slot_range = jnp.arange(slots_here, dtype=jnp.int32)
     in_use = slot_range < my_count
     gathered_cols, gathered_bonds = (
-        lax.all_gather(ham_columns, "sub", axis=0, tiled=True),
+        gather_by_exchange(ham_columns, "sub", 0),
         lax.all_gather(bond_mask, "sub", axis=0, tiled=True),
     )
     group_counts = lax.dynamic_index_in_dim(owned_counts, group_index, 0, keepdims=False)

time: 374 us -> 393 us (1.051)
  blocking collectives: 14.4 us -> 51 us
  waiting for transfers between devices: 37.6 us -> 14.3 us
  between operations: 14.1 us -> 0.75 us
  local copies, waits for them, and re-layouts: 54.5 us -> 66.6 us
  starting transfers between devices: 11.4 us -> 19.8 us
    all_gather x1, blocking collectives: 14.4 us -> 51 us  [body(): lax.all_gather(bond_mask, 'sub', axis=0, tiled=True)]
    all_gather x1 -> x0, waiting for transfers between devices: 22.8 us -> none  [body(): lax.all_gather(ham_columns, 'sub', axis=0, tiled=True)]
    unnamed x4 -> x15, local copies, waits for them, and re-layouts: 0.09 us -> 12.2 us
    all_to_all x0 -> x1, starting transfers between devices: none -> 7.6 us  [gather_by_exchange(): return lax.all_to_all(copies, axis, dim, dim, tiled=True)]
  transfers between devices with their start and end apart: 6 -> 6, of which waited for: 3 -> 2; matrix products, arithmetic and copies ran while one was open for 1% -> 1% of each run, Pallas kernels for 0% -> 0%
where the time goes in v1:
time: 393 us; the launch traced here: 386 us
  other arithmetic  116 us (30%)
  loops' own time  91.3 us (23%)
  local copies, waits for them, and re-layouts  66.6 us (17%)
  blocking collectives  51 us (13%)
  matrix products  26.7 us (7%)
  starting transfers between devices  19.8 us (5%)
  waiting for transfers between devices  14.3 us (4%)
    another operation x1, loops' own time, body(): lax.map(lambda first_row: window_result(edge_cols, edge_bonds, first_row,...  91.3 us
    while x84, other arithmetic  90.3 us
    all_gather x1, blocking collectives, body(): lax.all_gather(bond_mask, 'sub', axis=0, tiled=True)  51 us
    while x72, local copies, waits for them, and re-layouts  33.6 us
    dot_general x10, matrix products, product(): jnp.dot(matrix, vector.astype(jnp.bfloat16), preferred_element_type=jnp.f...  26.7 us
    unnamed x15, local copies, waits for them, and re-layouts  12.2 us
    ppermute x2, starting transfers between devices, extended(): after = lax.ppermute(leading, axis, down)  10.9 us
    ppermute x2, waiting for transfers between devices, extended(): after = lax.ppermute(leading, axis, down)  9.27 us
  transfers between devices with their start and end apart: 6, of which 2 were waited for; matrix products, arithmetic and copies ran while one was open for 1% of the time, Pallas kernels for 0%

profile of v1, /device:TPU:1, one launch (start us, length us, event | category | flops | bytes accessed | tf_op | source)
XLA Modules:
  0.0 386.2 jit_solution(9080683137967743074)
XLA Ops:
  0.0 1.9 constant_dynamic-update-slice_fusion.49
  1.9 1.9 constant_dynamic-update-slice_fusion.48
  3.8 1.9 constant_dynamic-update-slice_fusion.47
  5.7 1.9 constant_dynamic-update-slice_fusion.46
  7.5 1.9 constant_dynamic-update-slice_fusion.45
  9.4 1.9 constant_dynamic-update-slice_fusion.44
  12.9 7.6 %all-to-all-start = ((bf16[24,5,128,128]{3,2,1,0:T(8,128)(2,1)}), bf16[24,5,128,128]{3,2,1,0:T(8,128)(2,1)}, u32[]{:S(2)}, u32[]{:S(2)}) async-start(bf16[24,5,128,128]{3,2,1,0:T(8,128)(2,1)} %constant_dynamic-update-slice_fusion.42), calls=%async_computation | async-start | bytes 7864320 | tf_op jit(solution)/shard_map/all_to_all | solution.py:12
  20.9 51.0 %all-gather = s32[8,3,4]{2,1,0:T(4,128)S(1)} all-gather(s32[1,3,4]{2,1,0:T(4,128)S(1)} %bitcast.405), channel_id=1, replica_groups=mesh['grp'=32,'sub'=8] {'sub'}, dimensions={0}, use_global_device_ids=true | all-gather | bytes 432 | tf_op jit(solution)/shard_map/all_gather | solution.py:119
  73.3 4.5 %gather_fusion.1 = bf16[16,5,128,128]{3,2,1,0:T(8,128)(2,1)} fusion(bf16[24,5,128,128]{3,2,1,0:T(8,128)(2,1)} %all-to-all-done, s32[1024]{0:T(1024)S(1)} %pad_clamp_fusion.1), kind=kCustom, calls=%fused_computation.1 | custom fusion | bytes 5242944 | tf_op jit(solution)/shard_map/jit(_take)/gather | solution.py:128
  77.8 2.1 broadcast_select_fusion
  80.8 6.1 %collective-permute-start.1 = (bf16[4,5,128,128]{3,2,1,0:T(8,128)(2,1)}, bf16[4,5,128,128]{3,2,1,0:T(8,128)(2,1)}, u32[]{:S(2)}, u32[]{:S(2)}) collective-permute-start(bf16[4,5,128,128]{3,2,1,0:T(8,128)(2,1)} %get-tuple-element.119), channel_id=1, source_target_pairs={{8,0},{16,8},{24,16},{32,24},{40,32},{48,40},{56,48},{64,56},{72,6... | collective-permute-start | bytes 1966088 | tf_op jit(solution)/shard_map/ppermute | solution.py:23
  87.0 4.8 %collective-permute-start.3 = (s32[4,4]{1,0:T(4,128)S(1)}, s32[4,4]{1,0:T(4,128)S(1)}, u32[]{:S(2)}, u32[]{:S(2)}) collective-permute-start(s32[4,4]{1,0:T(4,128)S(1)} %get-tuple-element.121), channel_id=1, source_target_pairs={{8,0},{16,8},{24,16},{32,24},{40,32},{48,40},{56,48},{64,56},{72,6... | collective-permute-start | bytes 200 | tf_op jit(solution)/shard_map/ppermute | solution.py:23
  91.9 9.3 %collective-permute-done.3 = s32[4,4]{1,0:T(4,128)S(1)} collective-permute-done((s32[4,4]{1,0:T(4,128)S(1)}, s32[4,4]{1,0:T(4,128)S(1)}, u32[]{:S(2)}, u32[]{:S(2)}) %collective-permute-start.3) | collective-permute-done | bytes 96 | tf_op jit(solution)/shard_map/ppermute | solution.py:23
  101.3 5.0 %collective-permute-done.2 = s32[4,4]{1,0:T(4,128)S(1)} collective-permute-done((s32[4,4]{1,0:T(4,128)S(1)}, s32[4,4]{1,0:T(4,128)S(1)}, u32[]{:S(2)}, u32[]{:S(2)}) %collective-permute-start.2) | collective-permute-done | bytes 96 | tf_op jit(solution)/shard_map/ppermute | solution.py:22
  106.4 3.3 pad_maximum_fusion
  109.7 269.3 %while.10 = (s32[]{:T(128)}, bf16[2,9,128,128]{3,2,1,0:T(8,128)(2,1)}, s32[2]{0:T(128)S(1)}, bf16[24,5,128,128]{3,2,1,0:T(8,128)(2,1)}, f32[]{:T(128)}, /*index=...) while((s32[]{:T(128)}, ...), condition=%wide.region_3.4_spmd, body=%wide.region_2.3_spmd.sunk | while | flops 2726674432 | bytes 48746780 | solution.py:135
  114.1 2.1 constant_dynamic-update-slice_fusion.89
  138.1 1.4 constant_dynamic-update-slice_fusion.94
  139.5 2.1 fusion.119
  149.5 2.1 constant_dynamic-update-slice_fusion.98
  151.5 1.4 bitcast_dynamic-update-slice_fusion.44
  152.9 2.1 fusion.120
  185.1 1.4 constant_dynamic-update-slice_fusion.117
  186.6 1.4 bitcast_dynamic-update-slice_fusion.47
  188.0 1.4 bitcast_dynamic-update-slice_fusion.48
  189.4 1.4 bitcast_dynamic-update-slice_fusion.49
  190.8 2.0 fusion.122
  201.4 1.4 bitcast_dynamic-update-slice_fusion.54
  204.9 1.4 bitcast_dynamic-update-slice_fusion.56
  206.3 2.0 fusion.124
  211.2 1.4 bitcast_dynamic-update-slice_fusion.57
  216.1 2.1 fusion.126
  220.4 1.4 bitcast_dynamic-update-slice_fusion.60
  223.2 1.4 bitcast_dynamic-update-slice_fusion.62
  224.6 2.1 fusion.128
  226.7 2.9 multiply_convert_fusion.2
  230.2 3.3 fusion.130
  233.5 1.9 fusion.131
  236.3 3.3 fusion.132
  239.7 3.9 %fusion.133 = bf16[1152,128]{1,0:T(8,128)(2,1)S(1)} fusion(bf16[1152,1152]{1,0:T(8,128)(2,1)S(1)} %multiply_convert_fusion.2, f32[512,128]{1,0:T(8,128)S(1)} %broadcast.398, f32[128,128]{1,0:T(8,128)} %fusion.129, f32[1152,128]{1,0:T(8,128)} %fusion.132, f32[1152,128]{1,0:T(8,128)} %fusion.130), kind=kOutput, calls=%fused_computation.16.clone.1 | convolution fusion | flops 681394176 | bytes 4456448 | tf_op jit(solution)/shard_map/while/body/eval_jaxpr/dot_general | solution.py:74
  248.7 2.1 constant_dynamic-update-slice_fusion.89
  272.7 1.4 constant_dynamic-update-slice_fusion.94
  274.2 2.1 fusion.119
  284.1 2.1 constant_dynamic-update-slice_fusion.98
  286.2 1.4 bitcast_dynamic-update-slice_fusion.44
  287.6 2.1 fusion.120
  319.8 1.4 constant_dynamic-update-slice_fusion.117
  321.2 1.4 bitcast_dynamic-update-slice_fusion.47
  322.6 1.4 bitcast_dynamic-update-slice_fusion.48
  324.0 1.4 bitcast_dynamic-update-slice_fusion.49
  325.4 2.0 fusion.122
  339.6 1.4 bitcast_dynamic-update-slice_fusion.56
  341.0 2.0 fusion.124
  345.8 1.4 bitcast_dynamic-update-slice_fusion.57
  350.8 2.1 fusion.126
  355.1 1.4 bitcast_dynamic-update-slice_fusion.60
  357.9 1.4 bitcast_dynamic-update-slice_fusion.62
  359.3 2.1 fusion.128
  361.3 2.9 multiply_convert_fusion.2
  364.9 3.3 fusion.130
  368.2 1.9 fusion.131
  371.0 3.3 fusion.132
  374.3 3.9 %fusion.133 = bf16[1152,128]{1,0:T(8,128)(2,1)S(1)} fusion(bf16[1152,1152]{1,0:T(8,128)(2,1)S(1)} %multiply_convert_fusion.2, f32[512,128]{1,0:T(8,128)S(1)} %broadcast.398, f32[128,128]{1,0:T(8,128)} %fusion.129, f32[1152,128]{1,0:T(8,128)} %fusion.132, f32[1152,128]{1,0:T(8,128)} %fusion.130), kind=kOutput, calls=%fused_computation.16.clone.1 | convolution fusion | flops 681394176 | bytes 4456448 | tf_op jit(solution)/shard_map/while/body/eval_jaxpr/dot_general | solution.py:74
  383.0 1.5 maximum_select_fusion
  (232 shorter events, 94.6 us)
Async XLA Ops:
  0.0 11.3 %copy-start = (bf16[3,5,128,128]{3,2,1,0:T(8,128)(2,1)S(1)}, bf16[3,5,128,128]{3,2,1,0:T(8,128)(2,1)}, u32[]{:S(2)}) copy-start(bf16[3,5,128,128]{3,2,1,0:T(8,128)(2,1)} %param.6) | copy-start | bytes 1474564
  9.4 11.2 %copy-start.1 = (s32[32,8]{0,1:T(8,128)S(1)}, s32[32,8]{0,1:T(8,128)}, u32[]{:S(2)}) copy-start(s32[32,8]{0,1:T(8,128)} %param.8) | copy-start | bytes 3076
  9.4 11.5 %copy-start.2 = (s32[3,4]{1,0:T(4,128)S(1)}, s32[3,4]{1,0:T(4,128)}, u32[]{:S(2)}) copy-start(s32[3,4]{1,0:T(4,128)} %param.7) | copy-start | bytes 148
  12.9 60.4 %all-to-all-start = ((bf16[24,5,128,128]{3,2,1,0:T(8,128)(2,1)}), bf16[24,5,128,128]{3,2,1,0:T(8,128)(2,1)}, u32[]{:S(2)}, u32[]{:S(2)}) async-start(bf16[24,5,128,128]{3,2,1,0:T(8,128)(2,1)} %constant_dynamic-update-slice_fusion.42), calls=%async_computation | async-start | bytes 7864320 | tf_op jit(solution)/shard_map/all_to_all | solution.py:12
  80.8 25.6 %collective-permute-start.1 = (bf16[4,5,128,128]{3,2,1,0:T(8,128)(2,1)}, bf16[4,5,128,128]{3,2,1,0:T(8,128)(2,1)}, u32[]{:S(2)}, u32[]{:S(2)}) collective-permute-start(bf16[4,5,128,128]{3,2,1,0:T(8,128)(2,1)} %get-tuple-element.119), channel_id=1, source_target_pairs={{8,0},{16,8},{24,16},{32,24},{40,32},{48,40},{56,48},{64,56},{72,6... | collective-permute-start | bytes 1966088 | tf_op jit(solution)/shard_map/ppermute | solution.py:23
  86.9 19.5 %collective-permute-start = (bf16[4,5,128,128]{3,2,1,0:T(8,128)(2,1)S(1)}, bf16[4,5,128,128]{3,2,1,0:T(8,128)(2,1)}, u32[]{:S(2)}, u32[]{:S(2)}) collective-permute-start(bf16[4,5,128,128]{3,2,1,0:T(8,128)(2,1)S(1)} %get-tuple-element.118), channel_id=1, source_target_pairs={{0,8},{8,16},{16,24},{24,32},{32,40},{40,48},{48,56},{56,64},{64,7... | collective-permute-start | bytes 1966088 | tf_op jit(solution)/shard_map/ppermute | solution.py:22
  87.0 14.2 %collective-permute-start.3 = (s32[4,4]{1,0:T(4,128)S(1)}, s32[4,4]{1,0:T(4,128)S(1)}, u32[]{:S(2)}, u32[]{:S(2)}) collective-permute-start(s32[4,4]{1,0:T(4,128)S(1)} %get-tuple-element.121), channel_id=1, source_target_pairs={{8,0},{16,8},{24,16},{32,24},{40,32},{48,40},{56,48},{64,56},{72,6... | collective-permute-start | bytes 200 | tf_op jit(solution)/shard_map/ppermute | solution.py:23
  91.8 14.4 %collective-permute-start.2 = (s32[4,4]{1,0:T(4,128)S(1)}, s32[4,4]{1,0:T(4,128)S(1)}, u32[]{:S(2)}, u32[]{:S(2)}) collective-permute-start(s32[4,4]{1,0:T(4,128)S(1)} %get-tuple-element.120), channel_id=1, source_target_pairs={{0,8},{8,16},{16,24},{24,32},{32,40},{40,48},{48,56},{56,64},{64,7... | collective-permute-start | bytes 200 | tf_op jit(solution)/shard_map/ppermute | solution.py:22
  379.0 4.0 %collective-permute-start.4 = (bf16[2,9,128,128]{3,2,1,0:T(8,128)(2,1)}, bf16[2,9,128,128]{3,2,1,0:T(8,128)(2,1)S(1)}, u32[]{:S(2)}, u32[]{:S(2)}) collective-permute-start(bf16[2,9,128,128]{3,2,1,0:T(8,128)(2,1)} %get-tuple-element.37), channel_id=1, source_target_pairs={{0,1},{1,0},{2,3},{3,2},{4,5},{5,4},{6,7},{7,6},{8,9},{9,8},{10,11... | collective-permute-start | bytes 1769480 | tf_op jit(solution)/shard_map/ppermute | solution.py:31
